TPU v7x, 32 devices: a whole 2x2x4 slice. The times are simulated.
32 devices in a mesh: gz: 4 (over z), xy: 8 (over y, x, core).
Axes of the slice: x: 2, y: 2, z: 4, core: 2. Of those that a mesh axis runs over, the one named last changes fastest.
Arguments:
- volume: float32 [64, 384, 128], P('gz', 'xy'), may hold values from 0 to 1
- measured: float32 [2, 5, 80, 384], P(None, None, 'gz', 'xy'), may hold values from 0 to 1
- view_order: int32 [48], replicated, may hold values from 0 to 47, each once
Outputs:
- volume_out: float32 [64, 384, 128], P('gz', 'xy')
- residual: float32 [5, 80, 384], P(None, 'gz', 'xy')
Inputs may be any that keep to these rules, and one draw needn't show every extreme that they name: `view_order`: A permutation of the numbers 0 to 47.
All inputs are finite; a program needn't handle non-finite values.
Results may differ from a plain program's by a relative error of at most 0.00078.
Values may be sent and summed in bfloat16 or wider, within the bound.
A program may use at most 64 MiB of HBM per device.

v0:
```python
import math

import jax
import jax.numpy as jnp
from jax import lax
from jax.sharding import PartitionSpec as P

Z_DEV = 16
X_DEV = 48
COLS_DEV = 48
NY = 128
VIEWS = 5
SUBSETS = 2
ANGLES = 48
ROWS_DEV = 20


def padded(shard, sides, width):
    for axis, dim in sides:
        devices, length = (lax.axis_size(axis), shard.shape[dim])
        up = [(i, (i + 1) % devices) for i in range(devices - 1)]
        down = [(j, i) for i, j in up]
        last = lax.slice_in_dim(shard, length - width, length, axis=dim)
        leading = lax.slice_in_dim(shard, 0, width, axis=dim)
        before = lax.ppermute(last, axis, up)
        after = lax.ppermute(leading, axis, down)
        shard = jnp.concatenate([before, shard, after], axis=dim)
    return shard


def column_weights(view_angle, x_first, x_count, nx_all, ny_all, dc_all):
    x_coords = (
        jnp.asarray(x_first).astype(jnp.float32)
        + jnp.arange(x_count, dtype=jnp.float32)
        - (nx_all - 1) / 2.0
    )
    y_coords = jnp.arange(ny_all, dtype=jnp.float32) - (ny_all - 1) / 2.0
    cosine = jnp.cos(view_angle)
    sine_value = jnp.sin(view_angle)
    along_axis = x_coords[:, None] * cosine + y_coords[None, :] * sine_value
    depth_axis = y_coords[None, :] * cosine - x_coords[:, None] * sine_value
    source = 2.0 * nx_all
    position = (dc_all - 1) / 2.0 + 0.9 * (dc_all / nx_all) * along_axis * source / (
        source + depth_axis
    )
    position = (
        position.reshape(x_count // 8, 8, ny_all // 16, 16).transpose(0, 2, 1, 3).reshape(-1, 128)
    )
    lowest = jnp.min(position, axis=1)
    first_block = jnp.clip(jnp.floor(lowest / 64.0), 0, dc_all // 64 - 2).astype(jnp.int32)
    columns = (first_block * 64)[:, None] + jnp.arange(128, dtype=jnp.int32)[None, :]
    weights = jnp.maximum(
        0.0, 1.0 - jnp.abs(position[:, :, None] - columns[:, None, :].astype(position.dtype))
    )
    return (weights.astype(jnp.bfloat16), first_block)


def place_blocks(values, first_block, block_count):
    block_ids = jnp.arange(block_count, dtype=jnp.int32)
    low_onehot = (first_block[:, None] == block_ids[None, :]).astype(jnp.float32)
    high_onehot = (first_block[:, None] + 1 == block_ids[None, :]).astype(jnp.float32)
    result = jnp.einsum(
        "sb,skc->kbc", low_onehot, values[:, :, :64], precision=lax.Precision.HIGHEST
    )
    result = result + jnp.einsum(
        "sb,skc->kbc", high_onehot, values[:, :, 64:], precision=lax.Precision.HIGHEST
    )
    return result.reshape(values.shape[1], block_count * 64)


def row_weights(row_ids, slice_ids, dr_all, nz_all):
    position = (dr_all - 1) / 2.0 + 0.96 * (dr_all / nz_all) * (
        slice_ids.astype(jnp.float32) - (nz_all - 1) / 2.0
    )
    inside = ((row_ids >= 0) & (row_ids < dr_all)).astype(jnp.float32)
    hat = jnp.maximum(
        0.0, 1.0 - jnp.abs(position[None, :] - row_ids[:, None].astype(jnp.float32)) / 2.0
    )
    return hat * inside[:, None]


def local(volume, measured, view_order):
    count_gz = lax.axis_size("gz")
    count_xy = lax.axis_size("xy")
    nx_all = X_DEV * count_xy
    dc_all = COLS_DEV * count_xy
    dr_all = ROWS_DEV * count_gz
    nz_all = Z_DEV * count_gz
    block_count = dc_all // 64
    margin = Z_DEV * count_gz // 40 + 3
    gz_index = lax.axis_index("gz")
    x_first = lax.axis_index("xy") * X_DEV
    tiled = (
        volume.reshape(Z_DEV, X_DEV // 8, 8, NY // 16, 16)
        .transpose(1, 3, 0, 2, 4)
        .reshape(-1, Z_DEV, 128)
    )
    slice_ids = gz_index * Z_DEV + jnp.arange(Z_DEV, dtype=jnp.int32)
    near_rows = gz_index * ROWS_DEV - margin + jnp.arange(ROWS_DEV + 2 * margin, dtype=jnp.int32)
    back_weights = row_weights(near_rows, slice_ids, dr_all, nz_all)
    slice_total = jnp.sum(back_weights, axis=0)
    own_rows = gz_index * ROWS_DEV + jnp.arange(ROWS_DEV, dtype=jnp.int32)
    own_ray_rows = jnp.sum(
        row_weights(own_rows, jnp.arange(nz_all, dtype=jnp.int32), dr_all, nz_all), axis=1
    )
    residual = jnp.zeros((VIEWS, ROWS_DEV, COLS_DEV), jnp.float32)
    for subset in range(SUBSETS):
        chosen = view_order[subset * VIEWS : (subset + 1) * VIEWS]
        angles = 2.0 * math.pi * chosen.astype(jnp.float32) / ANGLES
        tiled_rounded = tiled.astype(jnp.bfloat16)

        def project(view_angle):
            weights, first_block = column_weights(view_angle, x_first, X_DEV, nx_all, NY, dc_all)
            column_sums = jnp.einsum(
                "szv,svc->szc", tiled_rounded, weights, preferred_element_type=jnp.float32
            )
            placed = place_blocks(column_sums, first_block, block_count)
            column_total = place_blocks(
                jnp.sum(weights, axis=1, dtype=jnp.float32)[:, None, :], first_block, block_count
            )
            return (weights, first_block, placed, column_total)

        weights_all, first_all, placed_all, column_all = lax.map(project, angles)
        summed = (
            lax.psum_scatter(placed_all, "xy", scatter_dimension=2, tiled=True),
            lax.psum_scatter(column_all, "xy", scatter_dimension=2, tiled=True),
        )
        extended = padded(summed[0], (("gz", 1),), margin)
        near_slices = gz_index * Z_DEV - margin + jnp.arange(Z_DEV + 2 * margin, dtype=jnp.int32)
        slab_weights = row_weights(own_rows, near_slices, dr_all, nz_all)
        proj_owned = jnp.einsum(
            "rz,vzc->vrc", slab_weights, extended, precision=lax.Precision.HIGHEST
        )
        column_owned = summed[1]
        rays_owned = own_ray_rows[None, :, None] * column_owned
        residual = measured[subset] - proj_owned / jnp.maximum(rays_owned, 1.0)
        residual_rounded = residual.astype(jnp.bfloat16)
        spread = lax.all_gather(residual_rounded, "xy", axis=2, tiled=True)
        residual_rows = padded(spread, (("gz", 1),), margin)
        smeared = jnp.einsum(
            "rz,vrc->vzc",
            back_weights,
            residual_rows,
            precision=lax.Precision.HIGHEST,
            preferred_element_type=jnp.float32,
        ).astype(jnp.bfloat16)

        def accumulate(totals, item):
            back_total, norm_total = totals
            weights, first_block, smeared_view = item
            pieces = smeared_view.reshape(Z_DEV, block_count, 64)
            window = jnp.concatenate(
                (jnp.take(pieces, first_block, axis=1), jnp.take(pieces, first_block + 1, axis=1)),
                axis=2,
            )
            back_total = back_total + jnp.einsum(
                "zsc,svc->szv", window, weights, preferred_element_type=jnp.float32
            )
            norm_total = (
                norm_total
                + slice_total[None, :, None]
                * jnp.sum(weights, axis=2, dtype=jnp.float32)[:, None, :]
            )
            return ((back_total, norm_total), None)

        empty = jnp.zeros(tiled.shape, jnp.float32)
        (back_total, norm_total), leftover = lax.scan(
            accumulate, (empty, empty), (weights_all, first_all, smeared)
        )
        tiled = tiled + back_total / jnp.maximum(norm_total, 1.0)
    volume_out = (
        tiled.reshape(X_DEV // 8, NY // 16, Z_DEV, 8, 16)
        .transpose(2, 0, 3, 1, 4)
        .reshape(Z_DEV, X_DEV, NY)
    )
    return (volume_out, residual)


def solution(mesh):
    in_specs = (P("gz", "xy", None), P(None, None, "gz", "xy"), P())
    out_specs = (P("gz", "xy", None), P(None, "gz", "xy"))
    return jax.shard_map(local, mesh=mesh, in_specs=in_specs, out_specs=out_specs, check_vma=False)
```

profile of v0, /device:TPU:0, one launch (start us, length us, event | category | flops | bytes accessed | tf_op | source)
XLA Modules:
  0.0 373.6 jit_solution(9005556711022432457)
XLA Ops:
  7.2 3.2 reshape.483
  10.4 2.4 copy.96
  13.8 5.1 %broadcast.903.clone = bf16[5,48,128,128]{3,2,1,0:T(8,128)(2,1)} broadcast(bf16[]{:T(256)} %constant.282.clone.1), dimensions={} | broadcast | bytes 7864322 | tf_op jit(solution)/shard_map/broadcast.78
  18.8 41.9 %while.62 = (s32[]{:T(128)}, bf16[5,48,128,128]{3,2,1,0:T(8,128)(2,1)}, s32[5,48]{1,0:T(8,128)S(1)}, f32[5,16,384]{2,1,0:T(8,128)S(1)}, f32[5,1,384]{2,1,0:T(1,1...) while((s32[]{:T(128)}, ...), condition=%wide.region_3.0_spmd, body=%wide.region_0.3_spmd.sunk | while | flops 46113424 | bytes 3851361 | solution.py:123
  21.5 1.9 fusion.206
  38.2 1.9 fusion.206
  46.6 1.9 fusion.206
  64.6 34.2 %reduce-scatter.13.cloned.1.call-done = f32[48,80]{1,0:T(8,128)} async-done(((f32[384,80]{1,0:T(8,128)}), f32[48,80]{1,0:T(8,128)}) %reduce-scatter.13.cloned.1.call-update) | async-done | bytes 15376
  99.7 3.4 collective-permute-start
  104.4 31.0 %reduce-scatter.15.cloned.1.call-done = f32[48,5]{1,0:T(8,128)} async-done(((f32[384,5]{1,0:T(8,128)}), f32[48,5]{1,0:T(8,128)}) %reduce-scatter.15.cloned.1.call-update) | async-done | bytes 976
  136.9 10.4 %all_gather.6 = bf16[5,20,384]{1,0,2:T(8,128)(2,1)S(1)} all-gather(bf16[5,20,48]{1,0,2:T(8,128)(2,1)S(1)} %copy.55), channel_id=1, replica_groups=mesh['gz'=4,'xy'=8] {'xy'}, dimensions={2}, use_global_device_ids=true | all-gather | bytes 86400 | tf_op jit(solution)/shard_map/all_gather | solution.py:138
  147.7 3.4 collective-permute-start.2
  152.8 3.9 %collective-permute-done.3 = bf16[5,4,384]{2,1,0:T(4,128)(2,1)S(1)} collective-permute-done((bf16[5,4,384]{2,1,0:T(4,128)(2,1)S(1)}, bf16[5,4,384]{2,1,0:T(4,128)(2,1)S(1)}, u32[]{:S(2)}, u32[]{:S(2)}) %collective-permute-start.3) | collective-permute-done | bytes 15392 | tf_op jit(solution)/shard_map/ppermute | solution.py:26
  157.0 30.0 %while.64 = (s32[]{:T(128)}, f32[48,16,128]{2,1,0:T(8,128)S(1)}, f32[48,16,128]{2,1,0:T(8,128)S(1)}, bf16[5,16,384]{2,1,0:T(8,128)(2,1)S(1)}, s32[5,48]{1,0:T(8,...) while((s32[]{:T(128)}, f32[48,16,128]{2,1,0:T(8,128)S(1)}, ...), condition=%wide.region_10.12_spmd.clone, body=%wide.region_8.11_spmd.clone.sunk | while | flops 27718260 | bytes 5834932 | solution.py:167
  158.6 2.4 fusion.229
  161.0 1.9 convert_reduce_fusion.10
  164.6 2.4 fusion.229
  167.0 1.9 convert_reduce_fusion.10
  170.6 2.4 fusion.229
  172.9 1.9 convert_reduce_fusion.10
  176.6 2.4 fusion.229
  178.9 1.9 convert_reduce_fusion.10
  182.6 2.4 fusion.229
  184.9 1.9 convert_reduce_fusion.10
  187.1 5.1 %broadcast.903 = bf16[5,48,128,128]{3,2,1,0:T(8,128)(2,1)} broadcast(bf16[]{:T(256)} %constant.282.clone.1), dimensions={} | broadcast | bytes 7864322 | tf_op jit(solution)/shard_map/broadcast.78
  192.1 41.9 %while.63 = (s32[]{:T(128)}, bf16[5,48,128,128]{3,2,1,0:T(8,128)(2,1)}, s32[5,48]{1,0:T(8,128)S(1)}, f32[5,16,384]{2,1,0:T(8,128)S(1)}, f32[5,1,384]{2,1,0:T(1,1...) while((s32[]{:T(128)}, ...), condition=%wide.region_14.16_spmd, body=%wide.region_11.15_spmd.sunk | while | flops 46113424 | bytes 3851361 | solution.py:123
  194.8 1.9 fusion.220
  211.5 1.9 fusion.220
  237.4 31.0 %reduce-scatter.17.cloned.1.call-done = f32[48,80]{1,0:T(8,128)} async-done(((f32[384,80]{1,0:T(8,128)}), f32[48,80]{1,0:T(8,128)}) %reduce-scatter.17.cloned.1.call-update) | async-done | bytes 15376
  269.4 3.4 collective-permute-start.4
  274.1 31.5 %reduce-scatter.19.cloned.1.call-done = f32[48,5]{1,0:T(8,128)} async-done(((f32[384,5]{1,0:T(8,128)}), f32[48,5]{1,0:T(8,128)}) %reduce-scatter.19.cloned.1.call-update) | async-done | bytes 976
  307.6 10.4 %all_gather.7 = bf16[5,20,384]{1,0,2:T(8,128)(2,1)S(1)} all-gather(bf16[5,20,48]{1,0,2:T(8,128)(2,1)S(1)} %copy.60), channel_id=1, replica_groups=mesh['gz'=4,'xy'=8] {'xy'}, dimensions={2}, use_global_device_ids=true | all-gather | bytes 86400 | tf_op jit(solution)/shard_map/all_gather | solution.py:138
  318.4 3.4 collective-permute-start.6
  323.4 4.1 %collective-permute-done.7 = bf16[5,4,384]{2,1,0:T(4,128)(2,1)S(1)} collective-permute-done((bf16[5,4,384]{2,1,0:T(4,128)(2,1)S(1)}, bf16[5,4,384]{2,1,0:T(4,128)(2,1)S(1)}, u32[]{:S(2)}, u32[]{:S(2)}) %collective-permute-start.7) | collective-permute-done | bytes 15392 | tf_op jit(solution)/shard_map/ppermute | solution.py:26
  327.7 30.0 %while.65 = (s32[]{:T(128)}, f32[48,16,128]{2,1,0:T(8,128)S(1)}, f32[48,16,128]{2,1,0:T(8,128)S(1)}, bf16[5,16,384]{2,1,0:T(8,128)(2,1)S(1)}, s32[5,48]{1,0:T(8,...) while((s32[]{:T(128)}, f32[48,16,128]{2,1,0:T(8,128)S(1)}, ...), condition=%wide.region_19.21_spmd.clone, body=%wide.region_17.20_spmd.clone.sunk | while | flops 27718260 | bytes 5834932 | solution.py:167
  329.3 2.4 fusion.232
  331.7 1.9 convert_reduce_fusion.11
  335.3 2.4 fusion.232
  337.7 1.9 convert_reduce_fusion.11
  341.3 2.4 fusion.232
  343.7 1.9 convert_reduce_fusion.11
  347.3 2.4 fusion.232
  349.7 1.9 convert_reduce_fusion.11
  353.3 2.4 fusion.232
  355.7 1.9 convert_reduce_fusion.11
  358.6 1.9 reshape.485
  360.5 3.5 copy.95
  364.0 3.1 reshape.486
  (400 shorter events, 96.9 us)
Async XLA Ops:
  7.2 91.6 %reduce-scatter.13.cloned.1.call-start = ((), (), s32[]{:S(2)}) async-start(), calls=%async_computation.4 | async-start | bytes 221184
  12.8 0.9 copy-start.1
  61.3 3.0 copy-start
  62.3 73.2 %reduce-scatter.15.cloned.1.call-start = ((), (), s32[]{:S(2)}) async-start(), calls=%async_computation.5 | async-start | bytes 221184
  64.1 204.3 %reduce-scatter.17.cloned.1.call-start = ((), (), s32[]{:S(2)}) async-start(), calls=%async_computation.6 | async-start | bytes 221184
  99.7 36.7 %collective-permute-start = (f32[5,4,48]{2,1,0:T(4,128)S(1)}, f32[5,4,48]{2,1,0:T(4,128)S(1)}, u32[]{:S(2)}, u32[]{:S(2)}) collective-permute-start(f32[5,4,48]{2,1,0:T(4,128)S(1)} %get-tuple-element.463), channel_id=1, source_target_pairs={{0,8},{8,16},{16,24},{1,9},{9,17},{17,25},{2,10},{10,18},{18,26},{... | collective-permute-start | bytes 11528 | tf_op jit(solution)/shard_map/ppermute | solution.py:25
  103.1 33.3 %collective-permute-start.1 = (f32[5,4,48]{2,1,0:T(4,128)S(1)}, f32[5,4,48]{2,1,0:T(4,128)S(1)}, u32[]{:S(2)}, u32[]{:S(2)}) collective-permute-start(f32[5,4,48]{2,1,0:T(4,128)S(1)} %get-tuple-element.464), channel_id=1, source_target_pairs={{8,0},{16,8},{24,16},{9,1},{17,9},{25,17},{10,2},{18,10},{26,18},{... | collective-permute-start | bytes 11528 | tf_op jit(solution)/shard_map/ppermute | solution.py:26
  147.7 5.1 %collective-permute-start.2 = (bf16[5,4,384]{2,1,0:T(4,128)(2,1)S(1)}, bf16[5,4,384]{2,1,0:T(4,128)(2,1)S(1)}, u32[]{:S(2)}, u32[]{:S(2)}) collective-permute-start(bf16[5,4,384]{2,1,0:T(4,128)(2,1)S(1)} %get-tuple-element.459), channel_id=1, source_target_pairs={{0,8},{8,16},{16,24},{1,9},{9,17},{17,25},{2,10},{10,18},{18,26},{... | collective-permute-start | bytes 46088 | tf_op jit(solution)/shard_map/ppermute | solution.py:25
  151.1 5.6 %collective-permute-start.3 = (bf16[5,4,384]{2,1,0:T(4,128)(2,1)S(1)}, bf16[5,4,384]{2,1,0:T(4,128)(2,1)S(1)}, u32[]{:S(2)}, u32[]{:S(2)}) collective-permute-start(bf16[5,4,384]{2,1,0:T(4,128)(2,1)S(1)} %get-tuple-element.460), channel_id=1, source_target_pairs={{8,0},{16,8},{24,16},{9,1},{17,9},{25,17},{10,2},{18,10},{26,18},{... | collective-permute-start | bytes 46088 | tf_op jit(solution)/shard_map/ppermute | solution.py:26
  235.6 70.0 %reduce-scatter.19.cloned.1.call-start = ((), (), s32[]{:S(2)}) async-start(), calls=%async_computation.7 | async-start | bytes 221184
  269.4 37.1 %collective-permute-start.4 = (f32[5,4,48]{2,1,0:T(4,128)S(1)}, f32[5,4,48]{2,1,0:T(4,128)S(1)}, u32[]{:S(2)}, u32[]{:S(2)}) collective-permute-start(f32[5,4,48]{2,1,0:T(4,128)S(1)} %get-tuple-element.461), channel_id=1, source_target_pairs={{0,8},{8,16},{16,24},{1,9},{9,17},{17,25},{2,10},{10,18},{18,26},{... | collective-permute-start | bytes 11528 | tf_op jit(solution)/shard_map/ppermute | solution.py:25
  272.8 33.7 %collective-permute-start.5 = (f32[5,4,48]{2,1,0:T(4,128)S(1)}, f32[5,4,48]{2,1,0:T(4,128)S(1)}, u32[]{:S(2)}, u32[]{:S(2)}) collective-permute-start(f32[5,4,48]{2,1,0:T(4,128)S(1)} %get-tuple-element.462), channel_id=1, source_target_pairs={{8,0},{16,8},{24,16},{9,1},{17,9},{25,17},{10,2},{18,10},{26,18},{... | collective-permute-start | bytes 11528 | tf_op jit(solution)/shard_map/ppermute | solution.py:26
  318.4 5.0 %collective-permute-start.6 = (bf16[5,4,384]{2,1,0:T(4,128)(2,1)S(1)}, bf16[5,4,384]{2,1,0:T(4,128)(2,1)S(1)}, u32[]{:S(2)}, u32[]{:S(2)}) collective-permute-start(bf16[5,4,384]{2,1,0:T(4,128)(2,1)S(1)} %get-tuple-element.457), channel_id=1, source_target_pairs={{0,8},{8,16},{16,24},{1,9},{9,17},{17,25},{2,10},{10,18},{18,26},{... | collective-permute-start | bytes 46088 | tf_op jit(solution)/shard_map/ppermute | solution.py:25
  321.8 5.6 %collective-permute-start.7 = (bf16[5,4,384]{2,1,0:T(4,128)(2,1)S(1)}, bf16[5,4,384]{2,1,0:T(4,128)(2,1)S(1)}, u32[]{:S(2)}, u32[]{:S(2)}) collective-permute-start(bf16[5,4,384]{2,1,0:T(4,128)(2,1)S(1)} %get-tuple-element.458), channel_id=1, source_target_pairs={{8,0},{16,8},{24,16},{9,1},{17,9},{25,17},{10,2},{18,10},{26,18},{... | collective-permute-start | bytes 46088 | tf_op jit(solution)/shard_map/ppermute | solution.py:26
Sparse Core Ops, SparseCore 0:
  62.4 36.3 reduce-scatter.12
  101.8 33.6 reduce-scatter.14
  235.7 32.7 reduce-scatter.16
  271.9 33.6 reduce-scatter.18
where the time goes:
time: 375 us; the launch traced here: 374 us
  waiting for transfers between devices  136 us (36%)
  local copies, waits for them, and re-layouts  62.4 us (17%)
  other arithmetic  55.8 us (15%)
  matrix products  49.2 us (13%)
  blocking collectives  20.7 us (6%)
  starting transfers between devices  19.3 us (5%)
  loops' own time  16 us (4%)
  between operations  14.2 us (4%)
    unnamed x8, waiting for transfers between devices  128 us
    dot_general x10, matrix products, accumulate(): jnp.einsum('zsc,svc->szv', window, weights, preferred_element_type=jnp.fl...  23.7 us
    all_gather x2, blocking collectives, local(): spread = lax.all_gather(residual_rounded, 'xy', axis=2, tiled=True)  20.7 us
    reduce_sum x10, other arithmetic, accumulate(): jnp.sum(weights, axis=2, dtype=jnp.float32)[:, None, :]  19.1 us
    dynamic_update_slice x10, other arithmetic, local(): weights_all, first_all, placed_all, column_all = lax.map(project, angles)  18.8 us
    another operation x2, loops' own time, local(): weights_all, first_all, placed_all, column_all = lax.map(project, angles)  15.2 us
    dot_general x10, matrix products, project(): jnp.einsum('szv,svc->szc', tiled_rounded, weights, preferred_element_type...  13.7 us
    ppermute x4, starting transfers between devices, padded(): before = lax.ppermute(last, axis, up)  13.6 us
  transfers between devices with their start and end apart: 12, of which 6 were waited for; matrix products, arithmetic and copies ran while one was open for 2% of the time, Pallas kernels for 0%

commit v1 on v0

v1 whole, which is shorter than its diff:
```python
import functools
import math

import jax
import jax.numpy as jnp
from jax import lax
from jax.experimental import pallas as pl
from jax.experimental.pallas import tpu as pltpu
from jax.sharding import PartitionSpec as P

VIEWS = 5
SUBSETS = 2
ANGLES = 48
TX = 8
TY = 16
WIN = 48
STEP = 16
LANES = 128
VROWS = 32
HI = lax.Precision.HIGHEST
MESH = pl.DeviceIdType.MESH
NT = (((1,), (1,)), ((), ()))


def hat(pos, rows):
    return jnp.maximum(0.0, 1.0 - jnp.abs(pos - rows) / 2.0)


def slice_position(z, dr_all, nz_all):
    return (dr_all - 1) / 2.0 + 0.96 * (dr_all / nz_all) * (z - (nz_all - 1) / 2.0)


def column_position(x, y, cosine, sine, nx_all, ny, dc_all):
    xc = x - (nx_all - 1) / 2.0
    yc = y - (ny - 1) / 2.0
    along = xc * cosine + yc * sine
    depth = yc * cosine - xc * sine
    source = 2.0 * nx_all
    return (dc_all - 1) / 2.0 + 0.9 * (dc_all / nx_all) * along * source / (source + depth)


def tile_swap(rows):
    lane = lax.broadcasted_iota(jnp.int32, rows[0].shape, 1)
    for bit in (1, 2, 4):
        high = ((lane // TY) & bit) != 0
        new = []
        for i in range(TX):
            if i & bit:
                new.append(jnp.where(high, rows[i], pltpu.roll(rows[i - bit], LANES - TY * bit, 1)))
            else:
                new.append(jnp.where(high, pltpu.roll(rows[i + bit], TY * bit, 1), rows[i]))
        rows = new
    return rows


def fill_positions(u_ref, geom_ref, subset, cfg):
    nx_all, ny, dc_all, x_dev = cfg
    tiles = u_ref.shape[1]
    tile = lax.broadcasted_iota(jnp.int32, (tiles, LANES), 0)
    lane = lax.broadcasted_iota(jnp.int32, (tiles, LANES), 1)
    per = ny // TY
    x = ((tile // per) * TX + lane // TY).astype(jnp.float32) + geom_ref[2 * VIEWS * SUBSETS]
    y = ((tile % per) * TY + lane % TY).astype(jnp.float32)
    for v in range(VIEWS):
        k = subset * VIEWS + v
        u_ref[v] = column_position(
            x, y, geom_ref[k], geom_ref[VIEWS * SUBSETS + k], nx_all, ny, dc_all
        )


def weights_for(u_ref, v, t, start):
    row = u_ref[v, pl.ds(t, 1), :] - start.astype(jnp.float32)
    col = lax.broadcasted_iota(jnp.int32, (WIN, LANES), 0).astype(jnp.float32)
    return jnp.maximum(0.0, 1.0 - jnp.abs(row - col)).astype(jnp.bfloat16)


def project_tile(tile, t, subset, starts_ref, u_ref, accs):
    z_dev = tile.shape[0]
    ones = jnp.where(
        lax.broadcasted_iota(jnp.int32, (z_dev, LANES), 0) == 0, 1.0, 0.0
    ).astype(jnp.bfloat16)
    a = jnp.concatenate([tile.astype(jnp.bfloat16), ones], axis=0)
    starts = [pl.multiple_of(starts_ref[subset * VIEWS + v, t], STEP) for v in range(VIEWS)]
    w = jnp.concatenate([weights_for(u_ref, v, t, starts[v]) for v in range(VIEWS)], axis=0)
    part = lax.dot_general(w, a, NT, preferred_element_type=jnp.float32)
    for v in range(VIEWS):
        where = pl.ds(starts[v], WIN)
        accs[v][where, : 2 * z_dev] += part[v * WIN : (v + 1) * WIN]


def clear(accs):
    for acc in accs:
        acc[...] = jnp.zeros_like(acc)


def combine(accs, part_ref, z_dev):
    total = jnp.zeros(part_ref.shape, jnp.float32)
    lane = lax.broadcasted_iota(jnp.int32, part_ref.shape, 1)
    for v in range(VIEWS):
        a = accs[v][...]
        s = jnp.where(lane < z_dev, a, 0.0)
        n = jnp.where(lane == z_dev, a, 0.0)
        total = total + (pltpu.roll(s, z_dev * v, 1) if v else s)
        total = total + pltpu.roll(n, z_dev * (VIEWS - 1) + v, 1)
    part_ref[...] = total


def forward_kernel(cfg, starts_ref, geom_ref, vol_ref, tiles_ref, part_ref, u_ref, *accs):
    nx_all, ny, dc_all, x_dev = cfg
    tiles, z_dev = tiles_ref.shape[:2]
    fill_positions(u_ref, geom_ref, 0, cfg)
    clear(accs)
    per = ny // TY
    for g in range(x_dev // TX):
        rows = [vol_ref[pl.ds(g * TX + i, z_dev, stride=x_dev), :] for i in range(TX)]
        rows = tile_swap(rows)
        for j in range(per):
            tiles_ref[g * per + j] = rows[j]

    @pl.loop(0, tiles)
    def _(t):
        project_tile(tiles_ref[t], t, 0, starts_ref, u_ref, accs)

    combine(accs, part_ref, z_dev)


def make_blocks(sm_ref, blk_ref, z_dev):
    k = sm_ref.shape[1]
    eye = (
        lax.broadcasted_iota(jnp.int32, (k, k), 0) == lax.broadcasted_iota(jnp.int32, (k, k), 1)
    ).astype(jnp.bfloat16)
    rows = lax.dot_general(eye, sm_ref[...], NT, preferred_element_type=jnp.float32)
    for s in range(blk_ref.shape[0]):
        cut = rows[: VIEWS * z_dev, s * STEP : s * STEP + WIN].astype(jnp.bfloat16)
        for v in range(VIEWS):
            blk_ref[s, v, :, :WIN] = cut[v * z_dev : (v + 1) * z_dev]


def back_tile(tile, t, subset, starts_ref, u_ref, blk_ref, slice_total):
    z_dev = tile.shape[0]
    ones = jnp.where(
        lax.broadcasted_iota(jnp.int32, (z_dev, WIN), 0) == 0, 1.0, 0.0
    ).astype(jnp.bfloat16)
    total = jnp.zeros((2 * z_dev, LANES), jnp.float32)
    for v in range(VIEWS):
        start = starts_ref[subset * VIEWS + v, t]
        w = weights_for(u_ref, v, t, start)
        a = jnp.concatenate([blk_ref[start // STEP, v][:, :WIN], ones], axis=0)
        total = total + jnp.dot(a, w, preferred_element_type=jnp.float32)
    norm = slice_total * total[z_dev : z_dev + 1]
    return tile + total[:z_dev] / jnp.maximum(norm, 1.0)


def slice_totals(geom_ref, z_dev, dr_all, nz_all):
    z = lax.broadcasted_iota(jnp.int32, (z_dev, LANES), 0).astype(jnp.float32)
    pos = slice_position(z + geom_ref[2 * VIEWS * SUBSETS + 1], dr_all, nz_all)
    total = jnp.zeros((z_dev, LANES), jnp.float32)
    for r in range(dr_all):
        total = total + hat(pos, float(r))
    return total


def back_kernel(cfg, rows_cfg, subset, starts_ref, geom_ref, tiles_ref, sm_ref, *rest):
    nx_all, ny, dc_all, x_dev = cfg
    dr_all, nz_all = rows_cfg
    tiles, z_dev = tiles_ref.shape[:2]
    last = subset == SUBSETS - 1
    if last:
        vol_ref, u_ref, blk_ref, new_ref = rest
    else:
        new_ref, part_ref, u_ref, blk_ref, u2_ref, *accs = rest
        fill_positions(u2_ref, geom_ref, subset + 1, cfg)
        clear(accs)
    fill_positions(u_ref, geom_ref, subset, cfg)
    make_blocks(sm_ref, blk_ref, z_dev)
    slice_total = slice_totals(geom_ref, z_dev, dr_all, nz_all)

    @pl.loop(0, tiles)
    def _(t):
        tile = back_tile(tiles_ref[t], t, subset, starts_ref, u_ref, blk_ref, slice_total)
        new_ref[t] = tile
        if not last:
            project_tile(tile, t, subset + 1, starts_ref, u2_ref, accs)

    if not last:
        combine(accs, part_ref, z_dev)
        return
    per = ny // TY
    for g in range(x_dev // TX):
        rows = tile_swap([new_ref[g * per + j] for j in range(per)])
        for i in range(TX):
            vol_ref[pl.ds(g * TX + i, z_dev, stride=x_dev), :] = rows[i]


def comm_kernel(dims, part_ref, meas_ref, sm_ref, *rest):
    n, ngz, z_dev, rows_dev, cols, margin = dims
    (res_ref, got, sums, nbr, mnbr, own, sa, ra, sb, rb, sm_sem, rm_sem, sc, rc) = rest
    nz_all, dr_all = z_dev * ngz, rows_dev * ngz
    gz, me = lax.axis_index("gz"), lax.axis_index("xy")
    peers = [lax.rem(me + k, n) for k in range(1, n)]
    sides = ((0, gz > 0, gz - 1), (1, gz < ngz - 1, gz + 1))

    barrier = pltpu.get_barrier_semaphore()
    for p in peers:
        pl.semaphore_signal(barrier, inc=1, device_id=(gz, p), device_id_type=MESH)
    for _, there, other in sides:

        @pl.when(there)
        def _():
            pl.semaphore_signal(barrier, inc=1, device_id=(other, me), device_id_type=MESH)

    near = lax.div(gz + ngz - 1, ngz) + lax.div(2 * ngz - 2 - gz, ngz)
    pl.semaphore_wait(barrier, n - 1 + near)

    first = []
    for k, p in enumerate(peers):
        copy = pltpu.make_async_remote_copy(
            src_ref=part_ref.at[pl.ds(pl.multiple_of(p * cols, 8), cols)],
            dst_ref=got.at[k],
            send_sem=sa.at[k],
            recv_sem=ra.at[k],
            device_id=(gz, p),
            device_id_type=MESH,
        )
        copy.start()
        first.append(copy)

    def side_copy(src, dst, side, other, send, recv):
        return pltpu.make_async_remote_copy(
            src_ref=src,
            dst_ref=dst.at[1 - side],
            send_sem=send.at[side],
            recv_sem=recv.at[1 - side],
            device_id=(other, me),
            device_id_type=MESH,
        )

    def side_wait(src, dst, side, other, send, recv):
        side_copy(src, dst, side, other, send, recv).wait_send()
        side_copy(src, dst, 1 - side, other, send, recv).wait_recv()

    for side, there, other in sides:

        @pl.when(there)
        def _():
            side_copy(meas_ref, mnbr, side, other, sm_sem, rm_sem).start()

    wide = 2 * LANES
    fz = gz.astype(jnp.float32)
    kk = lax.broadcasted_iota(jnp.int32, (LANES, wide), 0)
    ll = lax.broadcasted_iota(jnp.int32, (LANES, wide), 1)
    same = jnp.logical_and(kk // z_dev == ll // VROWS, kk < VIEWS * z_dev)
    ext = rows_dev + 2 * margin

    def row_of(lanes):
        rr = lanes % VROWS
        row = (rr - margin).astype(jnp.float32) + fz * rows_dev
        ok = (rr < ext) & (row >= 0) & (row < dr_all) & (lanes < VIEWS * VROWS)
        return rr, row, ok

    rr, row, ok = row_of(ll)
    keep = jnp.logical_and(same, ok)
    zz = (kk % z_dev).astype(jnp.float32)

    def slab(shift):
        z = zz + (fz + shift) * z_dev
        return jnp.where(keep, hat(slice_position(z, dr_all, nz_all), row), 0.0)

    mats = [slab(-1), slab(1), slab(0)]
    pick = (kk == VIEWS * z_dev + ll // VROWS).astype(jnp.float32)
    z_all = lax.broadcasted_iota(jnp.int32, (nz_all, wide), 0).astype(jnp.float32)
    _, row_all, _ = row_of(lax.broadcasted_iota(jnp.int32, (nz_all, wide), 1))
    ray_rows = jnp.sum(
        hat(slice_position(z_all, dr_all, nz_all), row_all), axis=0, keepdims=True
    )
    l2 = lax.broadcasted_iota(jnp.int32, (wide, LANES), 0)
    k2 = lax.broadcasted_iota(jnp.int32, (wide, LANES), 1)
    _, row2, ok2 = row_of(l2)
    keep2 = ok2 & (k2 // z_dev == l2 // VROWS) & (k2 < VIEWS * z_dev)
    z2 = (k2 % z_dev).astype(jnp.float32) + fz * z_dev
    back_mat = jnp.where(keep2, hat(slice_position(z2, dr_all, nz_all), row2), 0.0)

    total = part_ref[pl.ds(pl.multiple_of(me * cols, 8), cols), :]
    for k in range(n - 1):
        first[k].wait_recv()
        total = total + got[k]
    sums[...] = total
    for side, there, other in sides:

        @pl.when(there)
        def _():
            side_copy(sums, nbr, side, other, sb, rb).start()

    proj = jnp.dot(total, mats[2], precision=HI, preferred_element_type=jnp.float32)
    rays = ray_rows * jnp.dot(total, pick, precision=HI, preferred_element_type=jnp.float32)
    inverse = jnp.maximum(rays, 1.0)
    lc = lax.broadcasted_iota(jnp.int32, (cols, wide), 1)
    rc_row, _, rc_ok = row_of(lc)
    meas = meas_ref[...]

    for side, there, other in sides:

        @pl.when(there)
        def _():
            side_wait(meas_ref, mnbr, side, other, sm_sem, rm_sem)
            side_wait(sums, nbr, side, other, sb, rb)

        @pl.when(jnp.logical_not(there))
        def _():
            mnbr[side] = jnp.zeros_like(meas)
            nbr[side] = jnp.zeros_like(total)

    for side in range(2):
        proj = proj + jnp.dot(nbr[side], mats[side], precision=HI, preferred_element_type=jnp.float32)
    low = pltpu.roll(mnbr[0], wide - rows_dev, 1)
    high = pltpu.roll(mnbr[1], rows_dev, 1)
    meas = jnp.where(rc_row < margin, low, jnp.where(rc_row < margin + rows_dev, meas, high))
    residual = jnp.where(rc_ok, meas - proj / inverse, 0.0)
    res_ref[...] = residual
    rounded = residual.astype(jnp.bfloat16).astype(jnp.float32)
    smeared = jnp.dot(rounded, back_mat, precision=HI, preferred_element_type=jnp.float32)
    smeared = smeared.astype(jnp.bfloat16)
    own[...] = smeared
    mine = pl.ds(pl.multiple_of(me * cols, 16), cols)
    second = []
    for k, p in enumerate(peers):
        copy = pltpu.make_async_remote_copy(
            src_ref=own,
            dst_ref=sm_ref.at[mine],
            send_sem=sc.at[k],
            recv_sem=rc.at[k],
            device_id=(gz, p),
            device_id_type=MESH,
        )
        copy.start()
        second.append(copy)
    sm_ref[mine, :] = smeared
    for copy in first:
        copy.wait_send()
    for copy in second:
        copy.wait()


def local(ngz, n, volume, measured, view_order):
    z_dev, x_dev, ny = volume.shape
    rows_dev, cols = measured.shape[2:]
    nx_all, dc_all = x_dev * n, cols * n
    nz_all, dr_all = z_dev * ngz, rows_dev * ngz
    margin = nz_all // 40 + 3
    tiles = (x_dev // TX) * (ny // TY)
    count = VIEWS * SUBSETS
    gz, me = lax.axis_index("gz"), lax.axis_index("xy")
    cfg = (nx_all, ny, dc_all, x_dev)
    f32 = jnp.float32

    angles = 2.0 * math.pi * view_order[:count].astype(f32) / ANGLES
    cosine, sine = jnp.cos(angles), jnp.sin(angles)
    x_first = (me * x_dev).astype(f32)
    geom = jnp.concatenate(
        [cosine, sine, x_first[None], (gz * z_dev).astype(f32)[None]]
    )
    ids = jnp.arange(tiles, dtype=jnp.int32)
    tx = ((ids // (ny // TY)) * TX).astype(f32) + x_first
    ty = ((ids % (ny // TY)) * TY).astype(f32)
    lowest = None
    for dx in (0, TX - 1):
        for dy in (0, TY - 1):
            u = column_position(
                tx[None] + dx, ty[None] + dy, cosine[:, None], sine[:, None], nx_all, ny, dc_all
            )
            lowest = u if lowest is None else jnp.minimum(lowest, u)
    starts = jnp.clip(jnp.floor((lowest - 0.01) / STEP), 0, (dc_all - WIN) // STEP)
    starts = starts.astype(jnp.int32) * STEP

    meas_t = jnp.pad(
        measured.transpose(0, 3, 1, 2),
        ((0, 0), (0, 0), (0, 0), (margin, VROWS - margin - rows_dev)),
    ).reshape(SUBSETS, cols, VIEWS * VROWS)
    meas_t = jnp.pad(meas_t, ((0, 0), (0, 0), (0, 2 * LANES - VIEWS * VROWS)))

    smem = pl.BlockSpec(memory_space=pltpu.SMEM)
    vmem = pl.BlockSpec(memory_space=pltpu.VMEM)
    u_scr = pltpu.VMEM((VIEWS, tiles, LANES), f32)
    accs = [pltpu.VMEM((dc_all, LANES), f32) for _ in range(VIEWS)]
    tile_shape = jax.ShapeDtypeStruct((tiles, z_dev, LANES), f32)
    part_shape = jax.ShapeDtypeStruct((dc_all, LANES), f32)
    blocks = pltpu.VMEM(((dc_all - WIN) // STEP + 1, VIEWS, z_dev, LANES), jnp.bfloat16)

    tiled, part = pl.pallas_call(
        functools.partial(forward_kernel, cfg),
        out_shape=(tile_shape, part_shape),
        in_specs=[smem, smem, vmem],
        out_specs=(vmem, vmem),
        scratch_shapes=[u_scr, *accs],
    )(starts, geom, volume.reshape(z_dev * x_dev, ny))

    for subset in range(SUBSETS):
        last = subset == SUBSETS - 1
        dims = (n, ngz, z_dev, rows_dev, cols, margin)
        dma = pltpu.SemaphoreType.DMA
        smeared, residual = pl.pallas_call(
            functools.partial(comm_kernel, dims),
            out_shape=(
                jax.ShapeDtypeStruct((dc_all, LANES), jnp.bfloat16),
                jax.ShapeDtypeStruct((cols, 2 * LANES), f32),
            ),
            in_specs=[vmem, vmem],
            out_specs=(vmem, vmem),
            scratch_shapes=[
                pltpu.VMEM((n - 1, cols, LANES), f32),
                pltpu.VMEM((cols, LANES), f32),
                pltpu.VMEM((2, cols, LANES), f32),
                pltpu.VMEM((2, cols, 2 * LANES), f32),
                pltpu.VMEM((cols, LANES), jnp.bfloat16),
                dma((n - 1,)),
                dma((n - 1,)),
                dma((2,)),
                dma((2,)),
                dma((2,)),
                dma((2,)),
                dma((n - 1,)),
                dma((n - 1,)),
            ],
            compiler_params=pltpu.CompilerParams(collective_id=subset, has_side_effects=True),
        )(part, meas_t[subset])
        body = functools.partial(back_kernel, cfg, (dr_all, nz_all), subset)
        if last:
            volume_out = pl.pallas_call(
                body,
                out_shape=jax.ShapeDtypeStruct((z_dev * x_dev, ny), f32),
                in_specs=[smem, smem, vmem, vmem],
                out_specs=vmem,
                scratch_shapes=[u_scr, blocks, pltpu.VMEM(tile_shape.shape, f32)],
            )(starts, geom, tiled, smeared)
        else:
            tiled, part = pl.pallas_call(
                body,
                out_shape=(tile_shape, part_shape),
                in_specs=[smem, smem, vmem, vmem],
                out_specs=(vmem, vmem),
                scratch_shapes=[u_scr, blocks, u_scr, *accs],
            )(starts, geom, tiled, smeared)
    residual = residual[:, : VIEWS * VROWS].reshape(cols, VIEWS, VROWS)
    residual = residual[:, :, margin : margin + rows_dev].transpose(1, 2, 0)
    return (volume_out.reshape(z_dev, x_dev, ny), residual)


def solution(mesh):
    in_specs = (P("gz", "xy", None), P(None, None, "gz", "xy"), P())
    out_specs = (P("gz", "xy", None), P(None, "gz", "xy"))
    body = functools.partial(local, mesh.shape["gz"], mesh.shape["xy"])
    return jax.shard_map(body, mesh=mesh, in_specs=in_specs, out_specs=out_specs, check_vma=False)
```

time: 375 us -> 78.9 us (0.21)
  waiting for transfers between devices: 136 us -> 0 us
  Pallas kernels: 0 us -> 73.5 us
  local copies, waits for them, and re-layouts: 62.4 us -> 3.08 us
  other arithmetic: 55.8 us -> 1.37 us
  matrix products: 49.2 us -> 0 us
  blocking collectives: 20.7 us -> 0 us
  starting transfers between devices: 19.3 us -> 0 us
  loops' own time: 16 us -> 0 us
  between operations: 14.2 us -> 0.69 us
    unnamed x8 -> x0, waiting for transfers between devices: 128 us -> none
    pallas_call x0 -> x5, Pallas kernels: none -> 73.5 us  [the longest x2 32 us: local(): pl.pallas_call(functools.partial(comm_kernel, dims), out_shape=(jax.Shape...]
    dot_general x64 -> x0, matrix products: 49.2 us -> none  [the longest x10 23.7 us: accumulate(): jnp.einsum('zsc,svc->szv', window, weights, preferred_element_type=jnp.fl...]
    reduce_sum x22 -> x0, other arithmetic: 29.2 us -> none  [the longest x10 19.1 us: accumulate(): jnp.sum(weights, axis=2, dtype=jnp.float32)[:, None, :]]
    all_gather x2 -> x0, blocking collectives: 20.7 us -> none  [local(): spread = lax.all_gather(residual_rounded, 'xy', axis=2, tiled=True)]
    ppermute x8 -> x0, starting transfers between devices: 19.2 us -> none  [the longest x4 13.6 us: padded(): before = lax.ppermute(last, axis, up)]
    dynamic_update_slice x10 -> x0, other arithmetic: 18.8 us -> none  [local(): weights_all, first_all, placed_all, column_all = lax.map(project, angles)]
    another operation x4 -> x0, loops' own time: 16 us -> none  [the longest x2 15.2 us: local(): weights_all, first_all, placed_all, column_all = lax.map(project, angles)]
  transfers between devices with their start and end apart: 12 -> 0, of which waited for: 6 -> 0; matrix products, arithmetic and copies ran while one was open for 2% -> 0% of each run, Pallas kernels for 0% -> 0%
where the time goes in v1:
time: 78.9 us; the launch traced here: 78.6 us
  Pallas kernels  73.5 us (93%)
  local copies, waits for them, and re-layouts  3.08 us (4%)
  other arithmetic  1.37 us (2%)
    pallas_call x2, Pallas kernels, local(): pl.pallas_call(functools.partial(comm_kernel, dims), out_shape=(jax.Shape...  32 us
    pallas_call x1, Pallas kernels, local(): pl.pallas_call(body, out_shape=(tile_shape, part_shape), in_specs=[smem,...  19.8 us
    pallas_call x1, Pallas kernels, local(): pl.pallas_call(functools.partial(forward_kernel, cfg), out_shape=(tile_sh...  11.1 us
    pallas_call x1, Pallas kernels, local(): pl.pallas_call(body, out_shape=jax.ShapeDtypeStruct((z_dev * x_dev, ny),...  10.7 us

profile of v1, /device:TPU:0, one launch (start us, length us, event | category | flops | bytes accessed | tf_op | source)
XLA Modules:
  0.0 78.6 jit_solution(2959840432369592767)
XLA Ops:
  0.6 0.0 copy-start.1
  0.6 0.6 copy-done.1
  1.3 0.6 pad_maximum_fusion.geom_ref
  2.0 0.7 fusion.25.starts_ref
  2.7 0.9 %pad.8 = f32[2,48,5,32]{1,0,3,2:T(2,128)S(1)} pad(f32[2,48,5,20]{1,0,3,2:T(2,128)} %bitcast.18, f32[]{:T(128)} %constant.67.clone.1), padding=0_0x0_0x0_0x4_8 | pad | bytes 99844 | tf_op jit(solution)/shard_map/jit(_pad)/pad | solution.py:375
  3.6 0.1 copy.8
  3.7 0.6 fusion.1
  4.4 11.1 %shard_map.50 = (f32[48,16,128]{2,1,0:T(8,128)}, f32[384,128]{1,0:T(8,128)}) custom-call(s32[10,48]{1,0:T(8,128)} %fusion.25.starts_ref, f32[22]{0:T(128)} %pad_maximum_fusion.geom_ref, f32[768,128]{1,0:T(8,128)} %bitcast.15), custom_call_target="tpu_custom_call" | custom-call | tf_op jit(solution)/shard_map/pallas_call | solution.py:389
  15.5 17.3 %shard_map.51 = (bf16[384,128]{1,0:T(8,128)(2,1)}, f32[48,256]{1,0:T(8,128)}) custom-call(f32[384,128]{1,0:T(8,128)} %get-tuple-element.10.part_ref, f32[48,256]{1,0:T(8,128)} %get-tuple-element.17.meas_ref), custom_call_target="tpu_custom_call" | custom-call | tf_op jit(solution)/shard_map/pallas_call | solution.py:401
  32.8 19.8 %shard_map.52 = (f32[48,16,128]{2,1,0:T(8,128)}, f32[384,128]{1,0:T(8,128)}) custom-call(s32[10,48]{1,0:T(8,128)} %fusion.25.starts_ref, f32[22]{0:T(128)} %pad_maximum_fusion.geom_ref, f32[48,16,128]{2,1,0:T(8,128)} %get-tuple-element.9.tiles_ref, bf16[384,128]{1,0:T(8,128)(2,1)} %get-tuple-element.11.sm_ref), custom_call_target="tpu_custom_call" | custom-call | tf_op jit(solution)/shard_map/pallas_call | solution.py:436
  52.6 14.7 %shard_map.53 = (bf16[384,128]{1,0:T(8,128)(2,1)}, f32[48,256]{1,0:T(8,128)}) custom-call(f32[384,128]{1,0:T(8,128)} %get-tuple-element.13.part_ref, f32[48,256]{1,0:T(8,128)} %get-tuple-element.16.meas_ref), custom_call_target="tpu_custom_call" | custom-call | tf_op jit(solution)/shard_map/pallas_call | solution.py:401
  67.2 0.0 copy-start
  67.2 10.7 %shard_map.54 = f32[768,128]{1,0:T(8,128)} custom-call(s32[10,48]{1,0:T(8,128)} %fusion.25.starts_ref, f32[22]{0:T(128)} %pad_maximum_fusion.geom_ref, f32[48,16,128]{2,1,0:T(8,128)} %get-tuple-element.12.tiles_ref, bf16[384,128]{1,0:T(8,128)(2,1)} %get-tuple-element.14.sm_ref), custom_call_target="tpu_custom_call" | custom-call | tf_op jit(solution)/shard_map/pallas_call | solution.py:428
  77.9 0.0 copy-done
  77.9 0.1 copy.9
  78.0 0.6 slice_bitcast_fusion
  (3 shorter events, 0.1 us)
Async XLA Ops:
  0.6 0.7 copy-start.1
  67.2 10.7 %copy-start = (f32[48,256]{1,0:T(8,128)S(1)}, f32[48,256]{1,0:T(8,128)}, u32[]{:S(2)}) copy-start(f32[48,256]{1,0:T(8,128)} %get-tuple-element.15) | copy-start | bytes 147460

commit v2 on v1

--- a/solution.py
+++ b/solution.py
@@ -16,6 +16,7 @@
 WIN = 48
 STEP = 16
 LANES = 128
+GROUP = 4
 VROWS = 32
 HI = lax.Precision.HIGHEST
 MESH = pl.DeviceIdType.MESH
@@ -74,7 +75,18 @@
     return jnp.maximum(0.0, 1.0 - jnp.abs(row - col)).astype(jnp.bfloat16)
 
 
-def project_tile(tile, t, subset, starts_ref, u_ref, accs):
+def project_tiles(group, first, subset, starts_ref, u_ref, accs):
+    z_dev = group[0].shape[0]
+    parts = [
+        project_tile(tile, first + i, subset, starts_ref, u_ref) for i, tile in enumerate(group)
+    ]
+    for starts, part in parts:
+        for v in range(VIEWS):
+            where = pl.ds(starts[v], WIN)
+            accs[v][where, : 2 * z_dev] += part[v * WIN : (v + 1) * WIN]
+
+
+def project_tile(tile, t, subset, starts_ref, u_ref):
     z_dev = tile.shape[0]
     ones = jnp.where(
         lax.broadcasted_iota(jnp.int32, (z_dev, LANES), 0) == 0, 1.0, 0.0
@@ -82,10 +94,7 @@
     a = jnp.concatenate([tile.astype(jnp.bfloat16), ones], axis=0)
     starts = [pl.multiple_of(starts_ref[subset * VIEWS + v, t], STEP) for v in range(VIEWS)]
     w = jnp.concatenate([weights_for(u_ref, v, t, starts[v]) for v in range(VIEWS)], axis=0)
-    part = lax.dot_general(w, a, NT, preferred_element_type=jnp.float32)
-    for v in range(VIEWS):
-        where = pl.ds(starts[v], WIN)
-        accs[v][where, : 2 * z_dev] += part[v * WIN : (v + 1) * WIN]
+    return starts, lax.dot_general(w, a, NT, preferred_element_type=jnp.float32)
 
 
 def clear(accs):
@@ -117,9 +126,11 @@
         for j in range(per):
             tiles_ref[g * per + j] = rows[j]
 
-    @pl.loop(0, tiles)
-    def _(t):
-        project_tile(tiles_ref[t], t, 0, starts_ref, u_ref, accs)
+    @pl.loop(0, tiles // GROUP)
+    def _(step):
+        first = step * GROUP
+        group = [tiles_ref[first + i] for i in range(GROUP)]
+        project_tiles(group, first, 0, starts_ref, u_ref, accs)
 
     combine(accs, part_ref, z_dev)
 
@@ -175,12 +186,19 @@
     make_blocks(sm_ref, blk_ref, z_dev)
     slice_total = slice_totals(geom_ref, z_dev, dr_all, nz_all)
 
-    @pl.loop(0, tiles)
-    def _(t):
-        tile = back_tile(tiles_ref[t], t, subset, starts_ref, u_ref, blk_ref, slice_total)
-        new_ref[t] = tile
+    @pl.loop(0, tiles // GROUP)
+    def _(step):
+        first = step * GROUP
+        group = [
+            back_tile(
+                tiles_ref[first + i], first + i, subset, starts_ref, u_ref, blk_ref, slice_total
+            )
+            for i in range(GROUP)
+        ]
+        for i, tile in enumerate(group):
+            new_ref[first + i] = tile
         if not last:
-            project_tile(tile, t, subset + 1, starts_ref, u2_ref, accs)
+            project_tiles(group, first, subset + 1, starts_ref, u2_ref, accs)
 
     if not last:
         combine(accs, part_ref, z_dev)

time: 78.9 us -> 58.4 us (0.74)
  Pallas kernels: 73.5 us -> 53 us
    pallas_call x1, Pallas kernels: 19.8 us -> 8.53 us  [local(): pl.pallas_call(body, out_shape=(tile_shape, part_shape), in_specs=[smem,...]
    pallas_call x1, Pallas kernels: 11.1 us -> 6.44 us  [local(): pl.pallas_call(functools.partial(forward_kernel, cfg), out_shape=(tile_sh...]
    pallas_call x1, Pallas kernels: 10.7 us -> 6.09 us  [local(): pl.pallas_call(body, out_shape=jax.ShapeDtypeStruct((z_dev * x_dev, ny),...]
where the time goes in v2:
time: 58.4 us; the launch traced here: 58.1 us
  Pallas kernels  53 us (91%)
  local copies, waits for them, and re-layouts  3.08 us (5%)
  other arithmetic  1.37 us (2%)
  between operations  0.69 us (1%)
    pallas_call x2, Pallas kernels, local(): pl.pallas_call(functools.partial(comm_kernel, dims), out_shape=(jax.Shape...  31.9 us
    pallas_call x1, Pallas kernels, local(): pl.pallas_call(body, out_shape=(tile_shape, part_shape), in_specs=[smem,...  8.53 us
    pallas_call x1, Pallas kernels, local(): pl.pallas_call(functools.partial(forward_kernel, cfg), out_shape=(tile_sh...  6.44 us
    pallas_call x1, Pallas kernels, local(): pl.pallas_call(body, out_shape=jax.ShapeDtypeStruct((z_dev * x_dev, ny),...  6.09 us

profile of v2, /device:TPU:0, one launch (start us, length us, event | category | flops | bytes accessed | tf_op | source)
XLA Modules:
  0.0 58.1 jit_solution(8587740060262859546)
XLA Ops:
  0.6 0.0 copy-start.1
  0.6 0.6 %copy-done.1 = s32[48]{0:T(128)S(1)} copy-done((s32[48]{0:T(128)S(1)}, s32[48]{0:T(128)}, u32[]{:S(2)}) %copy-start.1) | copy-done | bytes 216
  1.3 0.6 %pad_maximum_fusion.geom_ref = f32[22]{0:T(128)} fusion(f32[1]{0:T(128)} %bitcast.1, f32[1]{0:T(128)} %bitcast, f32[10]{0:T(128)S(1)} %get-tuple-element.19, f32[10]{0:T(128)S(1)} %get-tuple-element.18), kind=kLoop, calls=%fused_computation.48 | loop fusion | flops 66 | bytes 176 | tf_op jit(solution)/shard_map/concatenate | solution.py:377
  2.0 0.7 %fusion.25.starts_ref = s32[10,48]{1,0:T(8,128)} fusion(f32[48]{0:T(128)S(1)} %get-tuple-element.20, f32[48]{0:T(128)S(1)} %get-tuple-element.22, f32[10]{0:T(128)S(1)} %get-tuple-element.19, f32[48]{0:T(128)S(1)} %get-tuple-element.23, f32[10]{0:T(128)S(1)} %get-tuple-element.18, f32[48]{0:T(128)S(1)} %get-tuple-element.21), kind=kLoop, calls=%fused_computation.36 | loop fusion | flops 19680 | bytes 2768 | tf_op jit(solution)/shard_map/mul | solution.py:391
  2.7 0.9 %pad.8 = f32[2,48,5,32]{1,0,3,2:T(2,128)S(1)} pad(f32[2,48,5,20]{1,0,3,2:T(2,128)} %bitcast.18, f32[]{:T(128)} %constant.67.clone.1), padding=0_0x0_0x0_0x4_8 | pad | bytes 99844 | tf_op jit(solution)/shard_map/jit(_pad)/pad | solution.py:393
  3.6 0.1 copy.8
  3.7 0.6 %fusion.1 = (f32[48,256]{1,0:T(8,128)}, f32[48,256]{1,0:T(8,128)}) fusion(f32[2,48,160]{2,1,0:T(8,128)S(1)} %copy.8), kind=kLoop, calls=%fused_computation.4 | loop fusion | bytes 159744 | tf_op jit(solution)/shard_map/squeeze | solution.py:443
  4.4 6.4 %shard_map.50 = (f32[48,16,128]{2,1,0:T(8,128)}, f32[384,128]{1,0:T(8,128)}) custom-call(s32[10,48]{1,0:T(8,128)} %fusion.25.starts_ref, f32[22]{0:T(128)} %pad_maximum_fusion.geom_ref, f32[768,128]{1,0:T(8,128)} %bitcast.15), custom_call_target="tpu_custom_call" | custom-call | tf_op jit(solution)/shard_map/pallas_call | solution.py:407
  10.8 17.3 %shard_map.51 = (bf16[384,128]{1,0:T(8,128)(2,1)}, f32[48,256]{1,0:T(8,128)}) custom-call(f32[384,128]{1,0:T(8,128)} %get-tuple-element.10.part_ref, f32[48,256]{1,0:T(8,128)} %get-tuple-element.17.meas_ref), custom_call_target="tpu_custom_call" | custom-call | tf_op jit(solution)/shard_map/pallas_call | solution.py:419
  28.1 8.5 %shard_map.52 = (f32[48,16,128]{2,1,0:T(8,128)}, f32[384,128]{1,0:T(8,128)}) custom-call(s32[10,48]{1,0:T(8,128)} %fusion.25.starts_ref, f32[22]{0:T(128)} %pad_maximum_fusion.geom_ref, f32[48,16,128]{2,1,0:T(8,128)} %get-tuple-element.9.tiles_ref, bf16[384,128]{1,0:T(8,128)(2,1)} %get-tuple-element.11.sm_ref), custom_call_target="tpu_custom_call" | custom-call | tf_op jit(solution)/shard_map/pallas_call | solution.py:454
  36.6 14.6 %shard_map.53 = (bf16[384,128]{1,0:T(8,128)(2,1)}, f32[48,256]{1,0:T(8,128)}) custom-call(f32[384,128]{1,0:T(8,128)} %get-tuple-element.13.part_ref, f32[48,256]{1,0:T(8,128)} %get-tuple-element.16.meas_ref), custom_call_target="tpu_custom_call" | custom-call | tf_op jit(solution)/shard_map/pallas_call | solution.py:419
  51.3 0.0 copy-start
  51.3 6.1 %shard_map.54 = f32[768,128]{1,0:T(8,128)} custom-call(s32[10,48]{1,0:T(8,128)} %fusion.25.starts_ref, f32[22]{0:T(128)} %pad_maximum_fusion.geom_ref, f32[48,16,128]{2,1,0:T(8,128)} %get-tuple-element.12.tiles_ref, bf16[384,128]{1,0:T(8,128)(2,1)} %get-tuple-element.14.sm_ref), custom_call_target="tpu_custom_call" | custom-call | tf_op jit(solution)/shard_map/pallas_call | solution.py:446
  57.4 0.0 copy-done
  57.4 0.1 copy.9
  57.5 0.6 %slice_bitcast_fusion = f32[5,20,48]{2,1,0:T(8,128)} fusion(f32[48,5,32]{0,2,1:T(8,128)S(1)} %bitcast.17), kind=kLoop, calls=%fused_computation.2 | loop fusion | bytes 38400 | tf_op jit(solution)/shard_map/transpose | solution.py:462
  (3 shorter events, 0.1 us)
Async XLA Ops:
  0.6 0.7 %copy-start.1 = (s32[48]{0:T(128)S(1)}, s32[48]{0:T(128)}, u32[]{:S(2)}) copy-start(s32[48]{0:T(128)} %param.5) | copy-start | bytes 580
  51.3 6.1 %copy-start = (f32[48,256]{1,0:T(8,128)S(1)}, f32[48,256]{1,0:T(8,128)}, u32[]{:S(2)}) copy-start(f32[48,256]{1,0:T(8,128)} %get-tuple-element.15) | copy-start | bytes 147460

commit v3 on v2

--- a/solution.py
+++ b/solution.py
@@ -16,9 +16,8 @@
 WIN = 48
 STEP = 16
 LANES = 128
-GROUP = 4
+GROUP = 8
 VROWS = 32
-HI = lax.Precision.HIGHEST
 MESH = pl.DeviceIdType.MESH
 NT = (((1,), (1,)), ((), ()))
 
@@ -210,9 +209,27 @@
             vol_ref[pl.ds(g * TX + i, z_dev, stride=x_dev), :] = rows[i]
 
 
+def split3(x):
+    a = x.astype(jnp.bfloat16)
+    rest = x - a.astype(jnp.float32)
+    b = rest.astype(jnp.bfloat16)
+    return a, b, (rest - b.astype(jnp.float32)).astype(jnp.bfloat16)
+
+
+def split_dot(terms, mats):
+    m = terms[0].shape[0]
+    one = jnp.dot(jnp.concatenate(terms, axis=0), mats[0], preferred_element_type=jnp.float32)
+    two = jnp.dot(
+        jnp.concatenate(terms[:2], axis=0), mats[1], preferred_element_type=jnp.float32
+    )
+    three = jnp.dot(terms[0], mats[2], preferred_element_type=jnp.float32)
+    small = one[2 * m :] + two[m:] + three
+    return one[:m] + ((one[m : 2 * m] + two[:m]) + small)
+
+
 def comm_kernel(dims, part_ref, meas_ref, sm_ref, *rest):
     n, ngz, z_dev, rows_dev, cols, margin = dims
-    (res_ref, got, sums, nbr, mnbr, own, sa, ra, sb, rb, sm_sem, rm_sem, sc, rc) = rest
+    (res_ref, got, sums, nbr, mnbr, own, sa, ra, sb, rb, sm_sem, rm_sem, sc, rc, slabs, backs) = rest
     nz_all, dr_all = z_dev * ngz, rows_dev * ngz
     gz, me = lax.axis_index("gz"), lax.axis_index("xy")
     peers = [lax.rem(me + k, n) for k in range(1, n)]
@@ -284,8 +301,10 @@
         z = zz + (fz + shift) * z_dev
         return jnp.where(keep, hat(slice_position(z, dr_all, nz_all), row), 0.0)
 
-    mats = [slab(-1), slab(1), slab(0)]
-    pick = (kk == VIEWS * z_dev + ll // VROWS).astype(jnp.float32)
+    for i, shift in enumerate((-1, 1, 0)):
+        for j, term in enumerate(split3(slab(shift))):
+            slabs[i, j] = term
+    pick = jnp.where(kk == VIEWS * z_dev + ll // VROWS, 1.0, 0.0).astype(jnp.bfloat16)
     z_all = lax.broadcasted_iota(jnp.int32, (nz_all, wide), 0).astype(jnp.float32)
     _, row_all, _ = row_of(lax.broadcasted_iota(jnp.int32, (nz_all, wide), 1))
     ray_rows = jnp.sum(
@@ -297,6 +316,8 @@
     keep2 = ok2 & (k2 // z_dev == l2 // VROWS) & (k2 < VIEWS * z_dev)
     z2 = (k2 % z_dev).astype(jnp.float32) + fz * z_dev
     back_mat = jnp.where(keep2, hat(slice_position(z2, dr_all, nz_all), row2), 0.0)
+    for j, term in enumerate(split3(back_mat)):
+        backs[j] = term
 
     total = part_ref[pl.ds(pl.multiple_of(me * cols, 8), cols), :]
     for k in range(n - 1):
@@ -309,8 +330,10 @@
         def _():
             side_copy(sums, nbr, side, other, sb, rb).start()
 
-    proj = jnp.dot(total, mats[2], precision=HI, preferred_element_type=jnp.float32)
-    rays = ray_rows * jnp.dot(total, pick, precision=HI, preferred_element_type=jnp.float32)
+    terms = split3(total)
+    proj = split_dot(terms, [slabs[2, j] for j in range(3)])
+    three = jnp.dot(jnp.concatenate(terms, axis=0), pick, preferred_element_type=jnp.float32)
+    rays = ray_rows * (three[:cols] + (three[cols : 2 * cols] + three[2 * cols :]))
     inverse = jnp.maximum(rays, 1.0)
     lc = lax.broadcasted_iota(jnp.int32, (cols, wide), 1)
     rc_row, _, rc_ok = row_of(lc)
@@ -329,15 +352,15 @@
             nbr[side] = jnp.zeros_like(total)
 
     for side in range(2):
-        proj = proj + jnp.dot(nbr[side], mats[side], precision=HI, preferred_element_type=jnp.float32)
+        proj = proj + split_dot(split3(nbr[side]), [slabs[side, j] for j in range(3)])
     low = pltpu.roll(mnbr[0], wide - rows_dev, 1)
     high = pltpu.roll(mnbr[1], rows_dev, 1)
     meas = jnp.where(rc_row < margin, low, jnp.where(rc_row < margin + rows_dev, meas, high))
     residual = jnp.where(rc_ok, meas - proj / inverse, 0.0)
     res_ref[...] = residual
-    rounded = residual.astype(jnp.bfloat16).astype(jnp.float32)
-    smeared = jnp.dot(rounded, back_mat, precision=HI, preferred_element_type=jnp.float32)
-    smeared = smeared.astype(jnp.bfloat16)
+    rounded = residual.astype(jnp.bfloat16)
+    pieces = [jnp.dot(rounded, backs[j], preferred_element_type=jnp.float32) for j in range(3)]
+    smeared = (pieces[0] + (pieces[1] + pieces[2])).astype(jnp.bfloat16)
     own[...] = smeared
     mine = pl.ds(pl.multiple_of(me * cols, 16), cols)
     second = []
@@ -438,6 +461,8 @@
                 dma((2,)),
                 dma((n - 1,)),
                 dma((n - 1,)),
+                pltpu.VMEM((3, 3, LANES, 2 * LANES), jnp.bfloat16),
+                pltpu.VMEM((3, 2 * LANES, LANES), jnp.bfloat16),
             ],
             compiler_params=pltpu.CompilerParams(collective_id=subset, has_side_effects=True),
         )(part, meas_t[subset])

time: 58.4 us -> 54.5 us (0.933)
  Pallas kernels: 53 us -> 49.1 us
    pallas_call x1, Pallas kernels: 8.53 us -> 6.88 us  [local(): pl.pallas_call(body, out_shape=(tile_shape, part_shape), in_specs=[smem,...]
    pallas_call x1, Pallas kernels: 6.44 us -> 5.44 us  [local(): pl.pallas_call(functools.partial(forward_kernel, cfg), out_shape=(tile_sh...]
    pallas_call x1, Pallas kernels: 6.09 us -> 5.37 us  [local(): pl.pallas_call(body, out_shape=jax.ShapeDtypeStruct((z_dev * x_dev, ny),...]
where the time goes in v3:
time: 54.5 us; the launch traced here: 54.3 us
  Pallas kernels  49.1 us (90%)
  local copies, waits for them, and re-layouts  3.08 us (6%)
  other arithmetic  1.37 us (3%)
  between operations  0.69 us (1%)
    pallas_call x2, Pallas kernels, local(): pl.pallas_call(functools.partial(comm_kernel, dims), out_shape=(jax.Shape...  31.5 us
    pallas_call x1, Pallas kernels, local(): pl.pallas_call(body, out_shape=(tile_shape, part_shape), in_specs=[smem,...  6.88 us
    pallas_call x1, Pallas kernels, local(): pl.pallas_call(functools.partial(forward_kernel, cfg), out_shape=(tile_sh...  5.44 us
    pallas_call x1, Pallas kernels, local(): pl.pallas_call(body, out_shape=jax.ShapeDtypeStruct((z_dev * x_dev, ny),...  5.37 us

profile of v3, /device:TPU:0, one launch (start us, length us, event | category | flops | bytes accessed | tf_op | source)
XLA Modules:
  0.0 54.3 jit_solution(6500803655149940921)
XLA Ops:
  0.6 0.0 copy-start.1
  0.6 0.6 %copy-done.1 = s32[48]{0:T(128)S(1)} copy-done((s32[48]{0:T(128)S(1)}, s32[48]{0:T(128)}, u32[]{:S(2)}) %copy-start.1) | copy-done | bytes 216
  1.3 0.6 %pad_maximum_fusion.geom_ref = f32[22]{0:T(128)} fusion(f32[1]{0:T(128)} %bitcast.1, f32[1]{0:T(128)} %bitcast, f32[10]{0:T(128)S(1)} %get-tuple-element.19, f32[10]{0:T(128)S(1)} %get-tuple-element.18), kind=kLoop, calls=%fused_computation.48 | loop fusion | flops 66 | bytes 176 | tf_op jit(solution)/shard_map/concatenate | solution.py:400
  2.0 0.7 %fusion.25.starts_ref = s32[10,48]{1,0:T(8,128)} fusion(f32[48]{0:T(128)S(1)} %get-tuple-element.20, f32[48]{0:T(128)S(1)} %get-tuple-element.22, f32[10]{0:T(128)S(1)} %get-tuple-element.19, f32[48]{0:T(128)S(1)} %get-tuple-element.23, f32[10]{0:T(128)S(1)} %get-tuple-element.18, f32[48]{0:T(128)S(1)} %get-tuple-element.21), kind=kLoop, calls=%fused_computation.36 | loop fusion | flops 19680 | bytes 2768 | tf_op jit(solution)/shard_map/mul | solution.py:414
  2.7 0.9 %pad.8 = f32[2,48,5,32]{1,0,3,2:T(2,128)S(1)} pad(f32[2,48,5,20]{1,0,3,2:T(2,128)} %bitcast.18, f32[]{:T(128)} %constant.67.clone.1), padding=0_0x0_0x0_0x4_8 | pad | bytes 99844 | tf_op jit(solution)/shard_map/jit(_pad)/pad | solution.py:416
  3.6 0.1 copy.8
  3.7 0.6 %fusion.1 = (f32[48,256]{1,0:T(8,128)}, f32[48,256]{1,0:T(8,128)}) fusion(f32[2,48,160]{2,1,0:T(8,128)S(1)} %copy.8), kind=kLoop, calls=%fused_computation.4 | loop fusion | bytes 159744 | tf_op jit(solution)/shard_map/squeeze | solution.py:468
  4.4 5.4 %shard_map.50 = (f32[48,16,128]{2,1,0:T(8,128)}, f32[384,128]{1,0:T(8,128)}) custom-call(s32[10,48]{1,0:T(8,128)} %fusion.25.starts_ref, f32[22]{0:T(128)} %pad_maximum_fusion.geom_ref, f32[768,128]{1,0:T(8,128)} %bitcast.15), custom_call_target="tpu_custom_call" | custom-call | tf_op jit(solution)/shard_map/pallas_call | solution.py:430
  9.8 17.0 %shard_map.51 = (bf16[384,128]{1,0:T(8,128)(2,1)}, f32[48,256]{1,0:T(8,128)}) custom-call(f32[384,128]{1,0:T(8,128)} %get-tuple-element.10.part_ref, f32[48,256]{1,0:T(8,128)} %get-tuple-element.17.meas_ref), custom_call_target="tpu_custom_call" | custom-call | tf_op jit(solution)/shard_map/pallas_call | solution.py:442
  26.8 6.9 %shard_map.52 = (f32[48,16,128]{2,1,0:T(8,128)}, f32[384,128]{1,0:T(8,128)}) custom-call(s32[10,48]{1,0:T(8,128)} %fusion.25.starts_ref, f32[22]{0:T(128)} %pad_maximum_fusion.geom_ref, f32[48,16,128]{2,1,0:T(8,128)} %get-tuple-element.9.tiles_ref, bf16[384,128]{1,0:T(8,128)(2,1)} %get-tuple-element.11.sm_ref), custom_call_target="tpu_custom_call" | custom-call | tf_op jit(solution)/shard_map/pallas_call | solution.py:479
  33.7 14.4 %shard_map.53 = (bf16[384,128]{1,0:T(8,128)(2,1)}, f32[48,256]{1,0:T(8,128)}) custom-call(f32[384,128]{1,0:T(8,128)} %get-tuple-element.13.part_ref, f32[48,256]{1,0:T(8,128)} %get-tuple-element.16.meas_ref), custom_call_target="tpu_custom_call" | custom-call | tf_op jit(solution)/shard_map/pallas_call | solution.py:442
  48.2 0.0 copy-start
  48.2 5.4 %shard_map.54 = f32[768,128]{1,0:T(8,128)} custom-call(s32[10,48]{1,0:T(8,128)} %fusion.25.starts_ref, f32[22]{0:T(128)} %pad_maximum_fusion.geom_ref, f32[48,16,128]{2,1,0:T(8,128)} %get-tuple-element.12.tiles_ref, bf16[384,128]{1,0:T(8,128)(2,1)} %get-tuple-element.14.sm_ref), custom_call_target="tpu_custom_call" | custom-call | tf_op jit(solution)/shard_map/pallas_call | solution.py:471
  53.5 0.0 copy-done
  53.5 0.1 copy.9
  53.6 0.6 %slice_bitcast_fusion = f32[5,20,48]{2,1,0:T(8,128)} fusion(f32[48,5,32]{0,2,1:T(8,128)S(1)} %bitcast.17), kind=kLoop, calls=%fused_computation.2 | loop fusion | bytes 38400 | tf_op jit(solution)/shard_map/transpose | solution.py:487
  (3 shorter events, 0.1 us)
Async XLA Ops:
  0.6 0.7 %copy-start.1 = (s32[48]{0:T(128)S(1)}, s32[48]{0:T(128)}, u32[]{:S(2)}) copy-start(s32[48]{0:T(128)} %param.5) | copy-start | bytes 580
  48.2 5.4 %copy-start = (f32[48,256]{1,0:T(8,128)S(1)}, f32[48,256]{1,0:T(8,128)}, u32[]{:S(2)}) copy-start(f32[48,256]{1,0:T(8,128)} %get-tuple-element.15) | copy-start | bytes 147460
